TPU v7x, 32 devices: a whole 2x2x4 slice. The times are simulated.
32 devices in a mesh: gx: 4 (over y, x), gy: 4 (over z), gz: 2 (over core).
Axes of the slice: x: 2, y: 2, z: 4, core: 2. Of those that a mesh axis runs over, the one named last changes fastest.
Arguments:
- densities: float32 [7, 64, 128, 512], P(None, 'gz', 'gy', 'gx'), may hold values from -6 to 6
- residuals: float32 [7, 64, 128, 512], P(None, 'gz', 'gy', 'gx'), may hold values from -320 to 320
Outputs:
- new_density: float32 [64, 128, 512], P('gz', 'gy', 'gx')
- weights: float32 [7], replicated
All inputs are finite; a program needn't handle non-finite values.
Results may differ from a plain program's by a relative error of at most 0.000087.
Values sent between devices are 32-bit elements; how exact they have to be, the bound alone decides.
A program may use at most 64 MiB of HBM per device.

v0:
```python
import math

import jax
import jax.numpy as jnp
from jax import lax
from jax.sharding import PartitionSpec as P

SWEEPS = 3


shift_value = 0.15
mix_amount = 0.7


def extended(cells, sides, width):
    for axis, dim in sides:
        count = lax.axis_size(axis)
        head = lax.slice_in_dim(cells, 0, width, axis=dim)
        tail = lax.slice_in_dim(cells, cells.shape[dim] - width, cells.shape[dim], axis=dim)
        cells = jnp.concatenate(
            [
                lax.ppermute(tail, axis, [(i, (i + 1) % count) for i in range(count)]),
                cells,
                lax.ppermute(head, axis, [((i + 1) % count, i) for i in range(count)]),
            ],
            axis=dim,
        )
    return cells


def sweep_weights():
    diag_value = 6.0 + shift_value
    upper = (shift_value + 12.0) / diag_value
    lower = upper / 3.0
    return [
        1.0
        / (
            (upper + lower) / 2.0
            + (upper - lower) / 2.0 * math.cos(math.pi * (2 * k - 1) / (2 * SWEEPS))
        )
        for k in range(1, SWEEPS + 1)
    ]


def neighbours(padded):
    total = padded[:, 2:, 1:-1, 1:-1] + padded[:, :-2, 1:-1, 1:-1]
    total = total + padded[:, 1:-1, 2:, 1:-1] + padded[:, 1:-1, :-2, 1:-1]
    return total + padded[:, 1:-1, 1:-1, 2:] + padded[:, 1:-1, 1:-1, :-2]


def shrink(field):
    return field[:, 1:-1, 1:-1, 1:-1]


def relax(padded, rhs, omega):
    diag_value = 6.0 + shift_value
    centre = shrink(padded)
    return centre + omega * (rhs - diag_value * centre + neighbours(padded)) / diag_value


def precondition(fields):
    diag_value = 6.0 + shift_value
    omegas = sweep_weights()
    padded = extended(fields, (("gx", 3), ("gy", 2), ("gz", 1)), SWEEPS)
    rhs = 6.0 * shrink(padded) - neighbours(padded)
    iterate = omegas[0] * rhs / diag_value
    for position in range(1, SWEEPS):
        rhs = shrink(rhs)
        iterate = relax(iterate, rhs, omegas[position])
    return iterate


def on_device(densities, residuals):
    count = residuals.shape[0]
    flat = residuals.reshape(count, -1)
    local = jnp.dot(
        flat, flat.T, precision=lax.Precision.HIGHEST, preferred_element_type=jnp.float32
    )
    gram = lax.psum(local, ("gx", "gy", "gz"))
    factor = jnp.linalg.cholesky(gram)
    ones_column = jnp.ones((count, 1), jnp.float32)
    middle = lax.linalg.triangular_solve(factor, ones_column, left_side=True, lower=True)
    solved = lax.linalg.triangular_solve(
        factor, middle, left_side=True, lower=True, transpose_a=True
    )[:, 0]
    weights = solved / jnp.sum(solved)
    blended = jnp.tensordot(weights, densities, axes=1, precision=lax.Precision.HIGHEST)
    combined = jnp.tensordot(weights, residuals, axes=1, precision=lax.Precision.HIGHEST)
    update = precondition(combined[None])[0]
    return (blended + mix_amount * update, weights)


def solution(mesh):
    placed = (P(None, "gz", "gy", "gx"), P(None, "gz", "gy", "gx"))
    return jax.shard_map(
        on_device, mesh=mesh, in_specs=placed, out_specs=(P("gz", "gy", "gx"), P()), check_vma=False
    )
```

profile of v0, /device:TPU:0, one launch (start us, length us, event | category | flops | bytes accessed | tf_op | source)
XLA Modules:
  0.0 116.0 jit_solution(11093563089816378523)
XLA Ops:
  0.6 14.5 %fusion.10 = f32[7,7]{0,1:T(8,128)S(1)} fusion(f32[7,32,32,128]{3,2,1,0:T(8,128)} %param.3), kind=kOutput, calls=%fused_computation.23 | convolution fusion | flops 77070336 | bytes 3670212 | tf_op jit(solution)/shard_map/dot_general | solution.py:76
  15.1 42.1 %psum.7 = f32[7,7]{0,1:T(8,128)S(1)} all-reduce(f32[7,7]{0,1:T(8,128)S(1)} %fusion.10), channel_id=1, replica_groups=mesh['gx'=4,'gy'=4,'gz'=2] {'gx','gy','gz'}, use_global_device_ids=true, to_apply=%region_0.0 | all-reduce | flops 49 | bytes 392 | tf_op jit(solution)/shard_map/psum | solution.py:79
  57.3 0.6 cholesky.16
  58.0 0.6 compare_reduce_fusion
  58.7 0.6 fusion.19
  59.3 0.5 custom-call.8
  60.0 0.8 fusion.29
  60.7 0.6 broadcast_divide_fusion
  61.4 7.8 %fusion = f32[1,32,32,128]{3,0,2,1:T(1,128)S(1)} fusion(f32[7,32,32,128]{3,2,1,0:T(8,128)} %param.3, f32[7]{0:T(128)S(1)} %broadcast_divide_fusion), kind=kOutput, calls=%fused_computation | convolution fusion | flops 11010048 | bytes 4194332 | tf_op jit(solution)/shard_map/dot_general | solution.py:88
  69.5 2.3 %collective-permute-start = (f32[1,32,32,3]{3,2,1,0:T(8,128)S(1)}, f32[1,32,32,3]{3,2,1,0:T(8,128)S(1)}, u32[]{:S(2)}, u32[]{:S(2)}) collective-permute-start(f32[1,32,32,3]{3,2,1,0:T(8,128)S(1)} %get-tuple-element.8), channel_id=1, source_target_pairs={{0,8},{8,16},{16,24},{24,0},{1,9},{9,17},{17,25},{25,1},{2,10},{10... | collective-permute-start | bytes 36872 | tf_op jit(solution)/shard_map/ppermute | solution.py:22
  71.8 0.6 collective-permute-start.1
  72.4 12.8 %collective-permute-done = f32[1,32,32,3]{3,2,1,0:T(8,128)S(1)} collective-permute-done((f32[1,32,32,3]{3,2,1,0:T(8,128)S(1)}, f32[1,32,32,3]{3,2,1,0:T(8,128)S(1)}, u32[]{:S(2)}, u32[]{:S(2)}) %collective-permute-start) | collective-permute-done | bytes 12320 | tf_op jit(solution)/shard_map/ppermute | solution.py:22
  85.2 9.2 %collective-permute-done.1 = f32[1,32,32,3]{3,2,1,0:T(8,128)S(1)} collective-permute-done((f32[1,32,32,3]{3,2,1,0:T(8,128)S(1)}, f32[1,32,32,3]{3,2,1,0:T(8,128)S(1)}, u32[]{:S(2)}, u32[]{:S(2)}) %collective-permute-start.1) | collective-permute-done | bytes 12320 | tf_op jit(solution)/shard_map/ppermute | solution.py:24
  94.4 0.3 pad_maximum_fusion.3
  94.7 1.6 %collective-permute-start.2 = (f32[1,32,3,134]{3,2,1,0:T(4,128)S(1)}, f32[1,32,3,134]{3,2,1,0:T(4,128)S(1)}, u32[]{:S(2)}, u32[]{:S(2)}) collective-permute-start(f32[1,32,3,134]{3,2,1,0:T(4,128)S(1)} %get-tuple-element.6), channel_id=1, source_target_pairs={{0,2},{2,4},{4,6},{6,0},{1,3},{3,5},{5,7},{7,1},{8,10},{10,12},{12... | collective-permute-start | bytes 154376 | tf_op jit(solution)/shard_map/ppermute | solution.py:22
  96.2 2.3 %collective-permute-start.3 = (f32[1,32,3,134]{3,2,1,0:T(4,128)S(1)}, f32[1,32,3,134]{3,2,1,0:T(4,128)S(1)}, u32[]{:S(2)}, u32[]{:S(2)}) collective-permute-start(f32[1,32,3,134]{3,2,1,0:T(4,128)S(1)} %get-tuple-element.7), channel_id=1, source_target_pairs={{2,0},{4,2},{6,4},{0,6},{3,1},{5,3},{7,5},{1,7},{10,8},{12,10},{14... | collective-permute-start | bytes 154376 | tf_op jit(solution)/shard_map/ppermute | solution.py:24
  98.5 3.0 %collective-permute-done.2 = f32[1,32,3,134]{3,2,1,0:T(4,128)S(1)} collective-permute-done((f32[1,32,3,134]{3,2,1,0:T(4,128)S(1)}, f32[1,32,3,134]{3,2,1,0:T(4,128)S(1)}, u32[]{:S(2)}, u32[]{:S(2)}) %collective-permute-start.2) | collective-permute-done | bytes 51488 | tf_op jit(solution)/shard_map/ppermute | solution.py:22
  101.6 1.0 collective-permute-done.3
  102.8 0.5 collective-permute-start.5
  103.4 5.2 %fusion.4 = f32[1,32,32,128]{3,0,2,1:T(1,128)S(1)} fusion(f32[7,32,32,128]{3,2,1,0:T(8,128)S(1)} %copy-done, f32[7]{0:T(128)S(1)} %broadcast_divide_fusion), kind=kOutput, calls=%fused_computation.4 | convolution fusion | flops 11010048 | bytes 4194332 | tf_op jit(solution)/shard_map/dot_general | solution.py:87
  108.6 0.6 pad_maximum_fusion
  109.2 2.3 %broadcast_multiply_fusion = (f32[1,36,36,132]{3,2,1,0:T(8,128)S(1)}, f32[1,36,36,132]{3,2,1,0:T(8,128)S(1)}) fusion(f32[1,38,38,134]{3,2,1,0:T(8,128)S(1)} %pad_maximum_fusion), kind=kLoop, calls=%fused_computation.26 | loop fusion | flops 1368576 | bytes 6158592 | tf_op jit(solution)/shard_map/div | solution.py:66
  111.5 2.6 %fusion.9 = f32[1,34,34,130]{3,2,1,0:T(8,128)S(1)} fusion(f32[1,36,36,132]{3,2,1,0:T(8,128)S(1)} %get-tuple-element.2, f32[1,36,36,132]{3,2,1,0:T(8,128)S(1)} %get-tuple-element.3), kind=kLoop, calls=%fused_computation.17 | loop fusion | flops 1502800 | bytes 5410080 | tf_op jit(solution)/shard_map/add | solution.py:58
  114.1 1.8 %fusion.18 = f32[32,32,128]{2,1,0:T(8,128)} fusion(f32[32,32,128]{2,1,0:T(8,128)S(1)} %bitcast.45, f32[1,34,34,130]{3,2,1,0:T(8,128)S(1)} %fusion.9, f32[1,36,36,132]{3,2,1,0:T(8,128)S(1)} %get-tuple-element.3), kind=kLoop, calls=%fused_computation.33 | loop fusion | flops 1572864 | bytes 5242880 | tf_op jit(solution)/shard_map/add | solution.py:90
  (13 shorter events, 0.7 us)
Async XLA Ops:
  61.4 42.0 %copy-start.1 = (f32[7]{0:T(128)}, f32[7]{0:T(128)S(1)}, u32[]{:S(2)}) copy-start(f32[7]{0:T(128)S(1)} %broadcast_divide_fusion) | copy-start | bytes 88
  69.5 15.7 %collective-permute-start = (f32[1,32,32,3]{3,2,1,0:T(8,128)S(1)}, f32[1,32,32,3]{3,2,1,0:T(8,128)S(1)}, u32[]{:S(2)}, u32[]{:S(2)}) collective-permute-start(f32[1,32,32,3]{3,2,1,0:T(8,128)S(1)} %get-tuple-element.8), channel_id=1, source_target_pairs={{0,8},{8,16},{16,24},{24,0},{1,9},{9,17},{17,25},{25,1},{2,10},{10... | collective-permute-start | bytes 36872 | tf_op jit(solution)/shard_map/ppermute | solution.py:22
  71.8 22.6 %collective-permute-start.1 = (f32[1,32,32,3]{3,2,1,0:T(8,128)S(1)}, f32[1,32,32,3]{3,2,1,0:T(8,128)S(1)}, u32[]{:S(2)}, u32[]{:S(2)}) collective-permute-start(f32[1,32,32,3]{3,2,1,0:T(8,128)S(1)} %get-tuple-element.9), channel_id=1, source_target_pairs={{8,0},{16,8},{24,16},{0,24},{9,1},{17,9},{25,17},{1,25},{10,2},{18... | collective-permute-start | bytes 36872 | tf_op jit(solution)/shard_map/ppermute | solution.py:24
  94.4 9.0 %copy-start = (f32[7,32,32,128]{3,2,1,0:T(8,128)S(1)}, f32[7,32,32,128]{3,2,1,0:T(8,128)}, u32[]{:S(2)}) copy-start(f32[7,32,32,128]{3,2,1,0:T(8,128)} %param.2) | copy-start | bytes 11010052
  94.7 6.9 %collective-permute-start.2 = (f32[1,32,3,134]{3,2,1,0:T(4,128)S(1)}, f32[1,32,3,134]{3,2,1,0:T(4,128)S(1)}, u32[]{:S(2)}, u32[]{:S(2)}) collective-permute-start(f32[1,32,3,134]{3,2,1,0:T(4,128)S(1)} %get-tuple-element.6), channel_id=1, source_target_pairs={{0,2},{2,4},{4,6},{6,0},{1,3},{3,5},{5,7},{7,1},{8,10},{10,12},{12... | collective-permute-start | bytes 154376 | tf_op jit(solution)/shard_map/ppermute | solution.py:22
  96.2 6.4 %collective-permute-start.3 = (f32[1,32,3,134]{3,2,1,0:T(4,128)S(1)}, f32[1,32,3,134]{3,2,1,0:T(4,128)S(1)}, u32[]{:S(2)}, u32[]{:S(2)}) collective-permute-start(f32[1,32,3,134]{3,2,1,0:T(4,128)S(1)} %get-tuple-element.7), channel_id=1, source_target_pairs={{2,0},{4,2},{6,4},{0,6},{3,1},{5,3},{7,5},{1,7},{10,8},{12,10},{14... | collective-permute-start | bytes 154376 | tf_op jit(solution)/shard_map/ppermute | solution.py:24
  102.8 5.8 %collective-permute-start.4 = (f32[1,3,38,134]{3,2,1,0:T(8,128)S(1)}, f32[1,3,38,134]{3,2,1,0:T(8,128)S(1)}, u32[]{:S(2)}, u32[]{:S(2)}) collective-permute-start(f32[1,3,38,134]{3,2,1,0:T(8,128)S(1)} %get-tuple-element.4), channel_id=1, source_target_pairs={{0,1},{1,0},{2,3},{3,2},{4,5},{5,4},{6,7},{7,6},{8,9},{9,8},{10,11... | collective-permute-start | bytes 183320 | tf_op jit(solution)/shard_map/ppermute | solution.py:22
  102.8 5.7 %collective-permute-start.5 = (f32[1,3,38,134]{3,2,1,0:T(8,128)S(1)}, f32[1,3,38,134]{3,2,1,0:T(8,128)S(1)}, u32[]{:S(2)}, u32[]{:S(2)}) collective-permute-start(f32[1,3,38,134]{3,2,1,0:T(8,128)S(1)} %get-tuple-element.5), channel_id=1, source_target_pairs={{1,0},{0,1},{3,2},{2,3},{5,4},{4,5},{7,6},{6,7},{9,8},{8,9},{11,10... | collective-permute-start | bytes 183320 | tf_op jit(solution)/shard_map/ppermute | solution.py:24
where the time goes:
time: 116 us
  blocking collectives  42.1 us (36%)
  matrix products  28.4 us (24%)
  waiting for transfers between devices  26 us (22%)
  other arithmetic  11 us (9%)
  starting transfers between devices  7.42 us (6%)
    psum x1, blocking collectives, on_device(): gram = lax.psum(local, ('gx', 'gy', 'gz'))  42.1 us
    ppermute x3, waiting for transfers between devices, extended(): lax.ppermute(tail, axis, [(i, (i + 1) % count) for i in range(count)])  15.8 us
    dot_general x1, matrix products, on_device(): jnp.dot(flat, flat.T, precision=lax.Precision.HIGHEST, preferred_element_...  14.5 us
    ppermute x3, waiting for transfers between devices, extended(): lax.ppermute(head, axis, [((i + 1) % count, i) for i in range(count)])  10.2 us
    dot_general x1, matrix products, on_device(): jnp.tensordot(weights, residuals, axes=1, precision=lax.Precision.HIGHEST)  7.85 us
    dot_general x1, matrix products, on_device(): jnp.tensordot(weights, densities, axes=1, precision=lax.Precision.HIGHEST)  5.18 us
    ppermute x3, starting transfers between devices, extended(): lax.ppermute(tail, axis, [(i, (i + 1) % count) for i in range(count)])  3.96 us
    ppermute x3, starting transfers between devices, extended(): lax.ppermute(head, axis, [((i + 1) % count, i) for i in range(count)])  3.46 us
  transfers between devices with their start and end apart: 6, of which 4 were waited for; matrix products, arithmetic and copies ran while one was open for 4% of the time, Pallas kernels for 0%

commit v1 on v0

v1 whole, which is shorter than its diff:
```python
import functools
import math

import jax
import jax.numpy as jnp
from jax import lax
from jax.experimental import pallas as pl
from jax.experimental.pallas import tpu as pltpu
from jax.sharding import PartitionSpec as P

MESH = pl.DeviceIdType.MESH
SWEEPS = 3
SUB = 8
shift_value = 0.15
mix_amount = 0.7
AXES = ("gx", "gy", "gz")


def sweep_weights():
    diag_value = 6.0 + shift_value
    upper = (shift_value + 12.0) / diag_value
    lower = upper / 3.0
    return [
        1.0
        / (
            (upper + lower) / 2.0
            + (upper - lower) / 2.0 * math.cos(math.pi * (2 * k - 1) / (2 * SWEEPS))
        )
        for k in range(1, SWEEPS + 1)
    ]


def kernel(
    counts, dims, chunks,
    res, den, out, wout,
    held, dens, slots, comb, side, rhs_a, rhs_b, it_a, it_b, zland, packs, landed,
    in_sem, den_sem, gsend, grecv, zsend, zrecv, ysend, yrecv, xsend, xrecv,
):
    count, nz, ny, nx = dims
    cx, cy, cz = counts
    total_devices = cx * cy * cz
    zp = nz + SUB
    h = SWEEPS
    ix, iy, iz = (lax.axis_index(a) for a in AXES)
    me = (ix * cy + iy) * cz + iz

    def coords(flat):
        return (flat // (cy * cz), lax.rem(flat // cz, cy), lax.rem(flat, cz))

    def near(dx, dy, dz):
        return (
            lax.rem(ix + dx + cx, cx),
            lax.rem(iy + dy + cy, cy),
            lax.rem(iz + dz + cz, cz),
        )

    per = nz // chunks
    loads = []
    for c in range(chunks):
        part = pl.ds(c * per, per)
        cp = pltpu.make_async_copy(res.at[:, part], held.at[:, part], in_sem.at[c])
        cp.start()
        loads.append(cp)
    den_load = pltpu.make_async_copy(den, dens, den_sem)
    den_load.start()

    barrier = pltpu.get_barrier_semaphore()

    @pl.loop(1, total_devices)
    def _(k):
        pl.semaphore_signal(
            barrier, inc=1, device_id=coords(lax.rem(me + k, total_devices)), device_id_type=MESH
        )

    pl.semaphore_wait(barrier, total_devices - 1)

    pairs = [(i, j) for i in range(count) for j in range(i, count)]
    tiles = ny // SUB
    accs = tuple(jnp.zeros((SUB, nx), jnp.float32) for _ in pairs)
    for c in range(chunks):
        loads[c].wait()

        def gram_step(z, accs):
            accs = list(accs)
            for t in range(tiles):
                v = [held[i, z, t * SUB:(t + 1) * SUB, :] for i in range(count)]
                for p, (i, j) in enumerate(pairs):
                    accs[p] = accs[p] + v[i] * v[j]
            return tuple(accs)

        accs = lax.fori_loop(c * per, (c + 1) * per, gram_step, accs)
    lane = lax.broadcasted_iota(jnp.int32, (SUB, nx), 1)
    packed = jnp.zeros((SUB, nx), jnp.float32)
    for p in range(len(pairs)):
        packed = jnp.where(lane == p, jnp.sum(accs[p], axis=1, keepdims=True), packed)
    slots[pl.ds(me, 1)] = jnp.sum(packed, axis=0, keepdims=True).reshape(1, 1, nx)

    def gram_copy(k, slot, target):
        return pltpu.make_async_remote_copy(
            src_ref=slots.at[me],
            dst_ref=slots.at[slot],
            send_sem=gsend.at[k],
            recv_sem=grecv.at[slot],
            device_id=coords(target),
            device_id_type=MESH,
        )

    @pl.loop(1, total_devices)
    def _(k):
        gram_copy(k, me, lax.rem(me + k, total_devices)).start()

    @pl.loop(1, total_devices)
    def _(k):
        other = lax.rem(me + k, total_devices)
        gram_copy(k, other, other).wait_recv()

    total = jnp.sum(slots[...], axis=0)

    g = {}
    for p, (i, j) in enumerate(pairs):
        g[i, j] = jnp.broadcast_to(total[:, p:p + 1], (SUB, nx))
    b = [jnp.ones((SUB, nx), jnp.float32) for _ in range(count)]
    inv = []
    for k in range(count):
        inv.append(1.0 / g[k, k])
        for i in range(k + 1, count):
            f = g[k, i] * inv[k]
            for j in range(i, count):
                g[i, j] = g[i, j] - f * g[k, j]
            b[i] = b[i] - f * b[k]
    solved = [None] * count
    for k in reversed(range(count)):
        s = b[k]
        for j in range(k + 1, count):
            s = s - g[k, j] * solved[j]
        solved[k] = s * inv[k]
    norm = solved[0]
    for k in range(1, count):
        norm = norm + solved[k]
    weights = [s / norm for s in solved]
    row = jnp.zeros((SUB, nx), jnp.float32)
    for k in range(count):
        row = jnp.where(lane == k, weights[k], row)
    wout[...] = row[0:1, :count]

    flat = comb.reshape((ny + 2 * h) * zp, nx)

    @pl.loop(0, nz)
    def _(z):
        for t in range(tiles):
            s = weights[0] * held[0, z, t * SUB:(t + 1) * SUB, :]
            for i in range(1, count):
                s = s + weights[i] * held[i, z, t * SUB:(t + 1) * SUB, :]
            flat[pl.ds((h + t * SUB) * zp + z, SUB, stride=zp), :] = s

    own = pl.ds(h, ny)
    zcopies = []
    for k, (start, dz) in enumerate(((0, -1), (nz - SUB, 1))):
        cp = pltpu.make_async_remote_copy(
            src_ref=comb.at[own, pl.ds(start, SUB)],
            dst_ref=zland.at[k],
            send_sem=zsend.at[k],
            recv_sem=zrecv.at[k],
            device_id=near(0, 0, dz),
            device_id_type=MESH,
        )
        cp.start()
        zcopies.append(cp)
    for cp in zcopies:
        cp.wait()
    sub = lax.broadcasted_iota(jnp.int32, (SUB, nx), 0)

    @pl.loop(0, ny, unroll=4)
    def _(y):
        comb[h + y, nz:zp, :] = jnp.where(sub < SUB // 2, zland[0, y], zland[1, y])

    ycopies = []
    for k, (start, dest, dy) in enumerate(((h, ny + h, -1), (ny, 0, 1))):
        cp = pltpu.make_async_remote_copy(
            src_ref=comb.at[pl.ds(start, h)],
            dst_ref=comb.at[pl.ds(dest, h)],
            send_sem=ysend.at[k],
            recv_sem=yrecv.at[k],
            device_id=near(0, dy, 0),
            device_id_type=MESH,
        )
        cp.start()
        ycopies.append(cp)

    group = lane // h

    @pl.loop(0, zp // SUB)
    def _(zt):
        rows = pl.ds(pl.multiple_of(zt * SUB, SUB), SUB)
        head = jnp.zeros((SUB, nx), jnp.float32)
        tail = jnp.zeros((SUB, nx), jnp.float32)
        for y in range(ny):
            v = comb[h + y, rows, :]
            here = group == y
            head = jnp.where(here, pltpu.roll(v, (h * y) % nx, 1), head)
            tail = jnp.where(here, pltpu.roll(v, (h * y + h) % nx, 1), tail)
        packs[0, rows, :] = head
        packs[1, rows, :] = tail

    xcopies = []
    for k, dx in enumerate((-1, 1)):
        for dy in (0, -1, 1):
            cp = pltpu.make_async_remote_copy(
                src_ref=packs.at[k],
                dst_ref=landed.at[k, 1 - dy],
                send_sem=xsend.at[k, 1 - dy],
                recv_sem=xrecv.at[k, 1 - dy],
                device_id=near(dx, dy, 0),
                device_id_type=MESH,
            )
            cp.start()
            xcopies.append(cp)

    den_load.wait()

    @pl.loop(0, nz)
    def _(z):
        for t in range(tiles):
            s = weights[0] * dens[0, z, t * SUB:(t + 1) * SUB, :]
            for i in range(1, count):
                s = s + weights[i] * dens[i, z, t * SUB:(t + 1) * SUB, :]
            out[z, t * SUB:(t + 1) * SUB, :] = s

    for cp in xcopies:
        cp.wait()

    @pl.loop(0, zp // SUB)
    def _(zt):
        rows = pl.ds(pl.multiple_of(zt * SUB, SUB), SUB)
        for e in range(ny + 2 * h):
            if e < h:
                slot, y = 0, ny - h + e
            elif e < ny + h:
                slot, y = 1, e - h
            else:
                slot, y = 2, e - h - ny
            head = pltpu.roll(landed[0, slot, rows, :], (-h * y) % nx, 1)
            tail = pltpu.roll(landed[1, slot, rows, :], (nx - h - h * y) % nx, 1)
            side[e, rows, :] = jnp.where(lane < nx // 2, head, tail)

    for cp in ycopies:
        cp.wait()

    wide = lax.broadcasted_iota(jnp.int32, (zp, nx), 1)
    first, last = wide == 0, wide == nx - 1

    def around(fa, fb, e, both):
        a, s = fa[e], fb[e]
        ra, rs = pltpu.roll(a, 1, 1), pltpu.roll(s, 1, 1)
        la, ls = pltpu.roll(a, nx - 1, 1), pltpu.roll(s, nx - 1, 1)
        na = jnp.where(first, rs, ra) + jnp.where(last, ls, la)
        na = na + (pltpu.roll(a, 1, 0) + pltpu.roll(a, zp - 1, 0))
        na = na + (fa[e - 1] + fa[e + 1])
        if not both:
            return a, na
        ns = jnp.where(first, ra, rs) + jnp.where(last, la, ls)
        ns = ns + (pltpu.roll(s, 1, 0) + pltpu.roll(s, zp - 1, 0))
        ns = ns + (fb[e - 1] + fb[e + 1])
        return a, na, s, ns

    diag_value = 6.0 + shift_value
    w1, w2, w3 = sweep_weights()
    alpha = ((1.0 - w2) * w1 + w2) / diag_value
    beta = w1 * w2 / (diag_value * diag_value)

    @pl.loop(1, ny + 2 * h - 1)
    def _(e):
        a, na, s, ns = around(comb, side, e, True)
        rhs_a[e] = 6.0 * a - na
        rhs_b[e] = 6.0 * s - ns

    @pl.loop(2, ny + 2 * h - 2)
    def _(e):
        a, na, s, ns = around(rhs_a, rhs_b, e, True)
        it_a[e] = alpha * a + beta * na
        it_b[e] = alpha * s + beta * ns

    out_flat = out.reshape(nz * ny, nx)

    @pl.loop(3, ny + 2 * h - 3)
    def _(e):
        a, na = around(it_a, it_b, e, False)
        u = (mix_amount * (1.0 - w3)) * a + (mix_amount * w3 / diag_value) * (rhs_a[e] + na)
        for zt in range(nz // SUB):
            rows = pl.ds(zt * SUB * ny + (e - h), SUB, stride=ny)
            out_flat[rows, :] = out_flat[rows, :] + u[zt * SUB:(zt + 1) * SUB, :]

    @pl.loop(1, total_devices)
    def _(k):
        gram_copy(k, me, lax.rem(me + k, total_devices)).wait_send()


def on_device(counts, densities, residuals):
    dims = residuals.shape
    count, nz, ny, nx = dims
    h = SWEEPS
    zp = nz + SUB
    n = counts[0] * counts[1] * counts[2]
    chunks = 4
    field = pltpu.VMEM((ny + 2 * h, zp, nx), jnp.float32)
    dma = pltpu.SemaphoreType.DMA
    any_spec = pl.BlockSpec(memory_space=pl.ANY)
    vmem = pl.BlockSpec(memory_space=pltpu.VMEM)
    new_density, weights = pl.pallas_call(
        functools.partial(kernel, counts, dims, chunks),
        out_shape=(
            jax.ShapeDtypeStruct((nz, ny, nx), jnp.float32),
            jax.ShapeDtypeStruct((1, count), jnp.float32),
        ),
        in_specs=[any_spec, any_spec],
        out_specs=(vmem, vmem),
        scratch_shapes=[
            pltpu.VMEM(dims, jnp.float32),
            pltpu.VMEM(dims, jnp.float32),
            pltpu.VMEM((n, 1, nx), jnp.float32),
            field, field, field, field, field, field,
            pltpu.VMEM((2, ny, SUB, nx), jnp.float32),
            pltpu.VMEM((2, zp, nx), jnp.float32),
            pltpu.VMEM((2, 3, zp, nx), jnp.float32),
            dma((chunks,)), dma(()), dma((n,)), dma((n,)),
            dma((2,)), dma((2,)), dma((2,)), dma((2,)), dma((2, 3)), dma((2, 3)),
        ],
        compiler_params=pltpu.CompilerParams(
            collective_id=0, has_side_effects=True, vmem_limit_bytes=61 * 1024 * 1024
        ),
    )(residuals, densities)
    return new_density, weights.reshape(count)


def solution(mesh):
    counts = tuple(mesh.shape[a] for a in AXES)
    placed = (P(None, "gz", "gy", "gx"), P(None, "gz", "gy", "gx"))
    return jax.shard_map(
        functools.partial(on_device, counts),
        mesh=mesh,
        in_specs=placed,
        out_specs=(P("gz", "gy", "gx"), P()),
        check_vma=False,
    )
```

time: 116 us -> 40.4 us (0.35)
  blocking collectives: 42.1 us -> 0 us
  Pallas kernels: 0 us -> 36.6 us
  matrix products: 28.4 us -> 0 us
  waiting for transfers between devices: 26 us -> 0 us
  other arithmetic: 11 us -> 0 us
  starting transfers between devices: 7.42 us -> 0 us
  local copies, waits for them, and re-layouts: 0.31 us -> 2.97 us
    psum x1 -> x0, blocking collectives: 42.1 us -> none  [on_device(): gram = lax.psum(local, ('gx', 'gy', 'gz'))]
    pallas_call x0 -> x1, Pallas kernels: none -> 36.6 us  [on_device(): pl.pallas_call(functools.partial(kernel, counts, dims, chunks), out_shape...]
    dot_general x3 -> x0, matrix products: 27.5 us -> none  [the longest x1 14.5 us: on_device(): jnp.dot(flat, flat.T, precision=lax.Precision.HIGHEST, preferred_element_...]
    ppermute x6 -> x0, waiting for transfers between devices: 26 us -> none  [the longest x3 15.8 us: extended(): lax.ppermute(tail, axis, [(i, (i + 1) % count) for i in range(count)])]
    ppermute x6 -> x0, starting transfers between devices: 7.42 us -> none  [the longest x3 3.96 us: extended(): lax.ppermute(tail, axis, [(i, (i + 1) % count) for i in range(count)])]
    add x2 -> x0, other arithmetic: 4.43 us -> none  [the longest x1 2.59 us: relax(): centre + omega * (rhs - diag_value * centre + neighbours(padded)) / diag_...]
    div x3 -> x0, other arithmetic: 3 us -> none  [the longest x1 2.35 us: precondition(): iterate = omegas[0] * rhs / diag_value]
    unnamed x4 -> x2, local copies, waits for them, and re-layouts: 0.01 us -> 2.97 us
  transfers between devices with their start and end apart: 6 -> 0, of which waited for: 4 -> 0; matrix products, arithmetic and copies ran while one was open for 4% -> 0% of each run, Pallas kernels for 0% -> 0%
where the time goes in v1:
time: 40.4 us; the launch traced here: 40.2 us
  Pallas kernels  36.6 us (91%)
  local copies, waits for them, and re-layouts  2.97 us (7%)
  between operations  0.64 us (2%)
    pallas_call x1, Pallas kernels, on_device(): pl.pallas_call(functools.partial(kernel, counts, dims, chunks), out_shape...  36.6 us
    unnamed x2, local copies, waits for them, and re-layouts  2.97 us

profile of v1, /device:TPU:0, one launch (start us, length us, event | category | flops | bytes accessed | tf_op | source)
XLA Modules:
  0.0 40.2 jit_solution(15451545454807340084)
XLA Ops:
  0.6 36.6 %shard_map.41 = (f32[32,32,128]{2,1,0:T(8,128)}, f32[1,7]{1,0:T(1,128)}) custom-call(f32[7,32,32,128]{3,2,1,0:T(8,128)} %res.1, f32[7,32,32,128]{3,2,1,0:T(8,128)} %den.1), custom_call_target="tpu_custom_call" | custom-call | tf_op jit(solution)/shard_map/pallas_call | solution.py:309
  37.3 1.9 %copy.6 = f32[32,32,128]{2,1,0:T(8,128)} copy(f32[32,32,128]{2,1,0:T(8,128)} %get-tuple-element.8) | data formatting | bytes 1048576
  39.1 1.1 %copy.7 = f32[7]{0:T(128)} copy(f32[7]{0:T(128)} %bitcast.1) | data formatting | bytes 56

commit v2 on v1

--- a/solution.py
+++ b/solution.py
@@ -11,6 +11,7 @@
 MESH = pl.DeviceIdType.MESH
 SWEEPS = 3
 SUB = 8
+UNROLL = 2
 shift_value = 0.15
 mix_amount = 0.7
 AXES = ("gx", "gy", "gz")
@@ -33,8 +34,8 @@
 def kernel(
     counts, dims, chunks,
     res, den, out, wout,
-    held, dens, slots, comb, side, rhs_a, rhs_b, it_a, it_b, zland, packs, landed,
-    in_sem, den_sem, gsend, grecv, zsend, zrecv, ysend, yrecv, xsend, xrecv,
+    held, dens, slots, comb, side, rhs_a, rhs_b, it_a, it_b, packs, landed, cpacks, clanded,
+    in_sem, den_sem, gsend, grecv, zsend, zrecv, ysend, yrecv, xsend, xrecv, csend, crecv,
 ):
     count, nz, ny, nx = dims
     cx, cy, cz = counts
@@ -57,8 +58,9 @@
     per = nz // chunks
     loads = []
     for c in range(chunks):
-        part = pl.ds(c * per, per)
-        cp = pltpu.make_async_copy(res.at[:, part], held.at[:, part], in_sem.at[c])
+        cp = pltpu.make_async_copy(
+            res.at[:, pl.ds(c * per, per)], held.at[:, pl.ds(h + c * per, per)], in_sem.at[c]
+        )
         cp.start()
         loads.append(cp)
     den_load = pltpu.make_async_copy(den, dens, den_sem)
@@ -72,7 +74,9 @@
             barrier, inc=1, device_id=coords(lax.rem(me + k, total_devices)), device_id_type=MESH
         )
 
-    pl.semaphore_wait(barrier, total_devices - 1)
+    @pl.loop(h, ny + h)
+    def _(y):
+        comb[y, nz:zp, :] = jnp.zeros((SUB, nx), jnp.float32)
 
     pairs = [(i, j) for i in range(count) for j in range(i, count)]
     tiles = ny // SUB
@@ -88,12 +92,14 @@
                     accs[p] = accs[p] + v[i] * v[j]
             return tuple(accs)
 
-        accs = lax.fori_loop(c * per, (c + 1) * per, gram_step, accs)
+        accs = lax.fori_loop(h + c * per, h + (c + 1) * per, gram_step, accs)
     lane = lax.broadcasted_iota(jnp.int32, (SUB, nx), 1)
     packed = jnp.zeros((SUB, nx), jnp.float32)
     for p in range(len(pairs)):
         packed = jnp.where(lane == p, jnp.sum(accs[p], axis=1, keepdims=True), packed)
     slots[pl.ds(me, 1)] = jnp.sum(packed, axis=0, keepdims=True).reshape(1, 1, nx)
+
+    pl.semaphore_wait(barrier, total_devices - 1)
 
     def gram_copy(k, slot, target):
         return pltpu.make_async_remote_copy(
@@ -108,6 +114,19 @@
     @pl.loop(1, total_devices)
     def _(k):
         gram_copy(k, me, lax.rem(me + k, total_devices)).start()
+
+    zcopies = []
+    for k, (start, dest, dz) in enumerate(((h, nz + h, -1), (nz, 0, 1))):
+        cp = pltpu.make_async_remote_copy(
+            src_ref=held.at[:, pl.ds(start, h)],
+            dst_ref=held.at[:, pl.ds(dest, h)],
+            send_sem=zsend.at[k],
+            recv_sem=zrecv.at[k],
+            device_id=near(0, 0, dz),
+            device_id_type=MESH,
+        )
+        cp.start()
+        zcopies.append(cp)
 
     @pl.loop(1, total_devices)
     def _(k):
@@ -145,34 +164,22 @@
 
     flat = comb.reshape((ny + 2 * h) * zp, nx)
 
-    @pl.loop(0, nz)
-    def _(z):
+    def combine(z, row):
         for t in range(tiles):
             s = weights[0] * held[0, z, t * SUB:(t + 1) * SUB, :]
             for i in range(1, count):
                 s = s + weights[i] * held[i, z, t * SUB:(t + 1) * SUB, :]
-            flat[pl.ds((h + t * SUB) * zp + z, SUB, stride=zp), :] = s
-
-    own = pl.ds(h, ny)
-    zcopies = []
-    for k, (start, dz) in enumerate(((0, -1), (nz - SUB, 1))):
-        cp = pltpu.make_async_remote_copy(
-            src_ref=comb.at[own, pl.ds(start, SUB)],
-            dst_ref=zland.at[k],
-            send_sem=zsend.at[k],
-            recv_sem=zrecv.at[k],
-            device_id=near(0, 0, dz),
-            device_id_type=MESH,
-        )
-        cp.start()
-        zcopies.append(cp)
+            flat[pl.ds((h + t * SUB) * zp + row, SUB, stride=zp), :] = s
+
+    @pl.loop(0, nz)
+    def _(z):
+        combine(z + h, z)
+
     for cp in zcopies:
         cp.wait()
-    sub = lax.broadcasted_iota(jnp.int32, (SUB, nx), 0)
-
-    @pl.loop(0, ny, unroll=4)
-    def _(y):
-        comb[h + y, nz:zp, :] = jnp.where(sub < SUB // 2, zland[0, y], zland[1, y])
+    for j in range(h):
+        combine(j, zp - h + j)
+        combine(nz + h + j, nz + j)
 
     ycopies = []
     for k, (start, dest, dy) in enumerate(((h, ny + h, -1), (ny, 0, 1))):
@@ -204,12 +211,32 @@
 
     xcopies = []
     for k, dx in enumerate((-1, 1)):
-        for dy in (0, -1, 1):
+        cp = pltpu.make_async_remote_copy(
+            src_ref=packs.at[k],
+            dst_ref=landed.at[k],
+            send_sem=xsend.at[k],
+            recv_sem=xrecv.at[k],
+            device_id=near(dx, 0, 0),
+            device_id_type=MESH,
+        )
+        cp.start()
+        xcopies.append(cp)
+    span = h * h
+    corner_group = lane // span
+    for k, dx in enumerate((-1, 1)):
+        for q, dy in enumerate((1, -1)):
+            first_lane = h * (ny - h) if dy > 0 else 0
+            corner = jnp.zeros((SUB, nx), jnp.float32)
+            for zt in range(zp // SUB):
+                v = packs[k, zt * SUB:(zt + 1) * SUB, :]
+                v = pltpu.roll(v, (span * zt - first_lane) % nx, 1)
+                corner = jnp.where(corner_group == zt, v, corner)
+            cpacks[k, q] = corner
             cp = pltpu.make_async_remote_copy(
-                src_ref=packs.at[k],
-                dst_ref=landed.at[k, 1 - dy],
-                send_sem=xsend.at[k, 1 - dy],
-                recv_sem=xrecv.at[k, 1 - dy],
+                src_ref=cpacks.at[k, q],
+                dst_ref=clanded.at[k, q],
+                send_sem=csend.at[k, q],
+                recv_sem=crecv.at[k, q],
                 device_id=near(dx, dy, 0),
                 device_id_type=MESH,
             )
@@ -229,19 +256,23 @@
     for cp in xcopies:
         cp.wait()
 
+    left = lane < nx // 2
+
     @pl.loop(0, zp // SUB)
     def _(zt):
         rows = pl.ds(pl.multiple_of(zt * SUB, SUB), SUB)
-        for e in range(ny + 2 * h):
-            if e < h:
-                slot, y = 0, ny - h + e
-            elif e < ny + h:
-                slot, y = 1, e - h
-            else:
-                slot, y = 2, e - h - ny
-            head = pltpu.roll(landed[0, slot, rows, :], (-h * y) % nx, 1)
-            tail = pltpu.roll(landed[1, slot, rows, :], (nx - h - h * y) % nx, 1)
-            side[e, rows, :] = jnp.where(lane < nx // 2, head, tail)
+        for y in range(ny):
+            head = pltpu.roll(landed[0, rows, :], (-h * y) % nx, 1)
+            tail = pltpu.roll(landed[1, rows, :], (nx - h - h * y) % nx, 1)
+            side[h + y, rows, :] = jnp.where(left, head, tail)
+
+    for q, base in ((0, 0), (1, ny + h)):
+        for zt in range(zp // SUB):
+            for r in range(h):
+                at = span * zt + h * r
+                head = pltpu.roll(clanded[0, q], (-at) % nx, 1)
+                tail = pltpu.roll(clanded[1, q], (nx - h - at) % nx, 1)
+                side[base + r, zt * SUB:(zt + 1) * SUB, :] = jnp.where(left, head, tail)
 
     for cp in ycopies:
         cp.wait()
@@ -268,13 +299,24 @@
     alpha = ((1.0 - w2) * w1 + w2) / diag_value
     beta = w1 * w2 / (diag_value * diag_value)
 
-    @pl.loop(1, ny + 2 * h - 1)
+    def planes(start, stop, unroll):
+        unroll = unroll if (stop - start) % unroll == 0 else 1
+
+        def wrap(body):
+            @pl.loop(0, (stop - start) // unroll)
+            def _(it):
+                for r in range(unroll):
+                    body(start + it * unroll + r)
+
+        return wrap
+
+    @planes(1, ny + 2 * h - 1, UNROLL)
     def _(e):
         a, na, s, ns = around(comb, side, e, True)
         rhs_a[e] = 6.0 * a - na
         rhs_b[e] = 6.0 * s - ns
 
-    @pl.loop(2, ny + 2 * h - 2)
+    @planes(2, ny + 2 * h - 2, UNROLL)
     def _(e):
         a, na, s, ns = around(rhs_a, rhs_b, e, True)
         it_a[e] = alpha * a + beta * na
@@ -282,7 +324,7 @@
 
     out_flat = out.reshape(nz * ny, nx)
 
-    @pl.loop(3, ny + 2 * h - 3)
+    @planes(3, ny + 2 * h - 3, UNROLL)
     def _(e):
         a, na = around(it_a, it_b, e, False)
         u = (mix_amount * (1.0 - w3)) * a + (mix_amount * w3 / diag_value) * (rhs_a[e] + na)
@@ -293,6 +335,13 @@
     @pl.loop(1, total_devices)
     def _(k):
         gram_copy(k, me, lax.rem(me + k, total_devices)).wait_send()
+
+
+def hand_over(mixed, weights, out, wout, sem):
+    cp = pltpu.make_async_copy(mixed, out, sem)
+    cp.start()
+    wout[...] = weights[...]
+    cp.wait()
 
 
 def on_device(counts, densities, residuals):
@@ -309,26 +358,38 @@
     new_density, weights = pl.pallas_call(
         functools.partial(kernel, counts, dims, chunks),
         out_shape=(
-            jax.ShapeDtypeStruct((nz, ny, nx), jnp.float32),
-            jax.ShapeDtypeStruct((1, count), jnp.float32),
+            pltpu.VMEM((nz, ny, nx), jnp.float32),
+            pltpu.VMEM((1, count), jnp.float32),
         ),
         in_specs=[any_spec, any_spec],
         out_specs=(vmem, vmem),
         scratch_shapes=[
-            pltpu.VMEM(dims, jnp.float32),
+            pltpu.VMEM((count, nz + 2 * h, ny, nx), jnp.float32),
             pltpu.VMEM(dims, jnp.float32),
             pltpu.VMEM((n, 1, nx), jnp.float32),
             field, field, field, field, field, field,
-            pltpu.VMEM((2, ny, SUB, nx), jnp.float32),
             pltpu.VMEM((2, zp, nx), jnp.float32),
-            pltpu.VMEM((2, 3, zp, nx), jnp.float32),
+            pltpu.VMEM((2, zp, nx), jnp.float32),
+            pltpu.VMEM((2, 2, SUB, nx), jnp.float32),
+            pltpu.VMEM((2, 2, SUB, nx), jnp.float32),
             dma((chunks,)), dma(()), dma((n,)), dma((n,)),
-            dma((2,)), dma((2,)), dma((2,)), dma((2,)), dma((2, 3)), dma((2, 3)),
+            dma((2,)), dma((2,)), dma((2,)), dma((2,)), dma((2,)), dma((2,)), dma((2, 2)), dma((2, 2)),
         ],
         compiler_params=pltpu.CompilerParams(
             collective_id=0, has_side_effects=True, vmem_limit_bytes=61 * 1024 * 1024
         ),
     )(residuals, densities)
+    new_density, weights = pl.pallas_call(
+        hand_over,
+        out_shape=(
+            jax.ShapeDtypeStruct((nz, ny, nx), jnp.float32),
+            jax.ShapeDtypeStruct((1, count), jnp.float32),
+        ),
+        in_specs=[vmem, vmem],
+        out_specs=(any_spec, vmem),
+        scratch_shapes=[dma(())],
+        compiler_params=pltpu.CompilerParams(vmem_limit_bytes=4 * 1024 * 1024),
+    )(new_density, weights)
     return new_density, weights.reshape(count)
 
 

time: 40.4 us -> 29.2 us (0.72)
  Pallas kernels: 36.6 us -> 28.4 us
  local copies, waits for them, and re-layouts: 2.97 us -> 0 us
    pallas_call x1, Pallas kernels: 36.6 us -> 27.1 us  [on_device(): pl.pallas_call(functools.partial(kernel, counts, dims, chunks), out_shape...]
    unnamed x2 -> x0, local copies, waits for them, and re-layouts: 2.97 us -> none
    pallas_call x0 -> x1, Pallas kernels: none -> 1.31 us  [on_device(): pl.pallas_call(hand_over, out_shape=(jax.ShapeDtypeStruct((nz, ny, nx), j...]
where the time goes in v2:
time: 29.2 us; the launch traced here: 29 us
  Pallas kernels  28.4 us (97%)
  between operations  0.64 us (2%)
    pallas_call x1, Pallas kernels, on_device(): pl.pallas_call(functools.partial(kernel, counts, dims, chunks), out_shape...  27.1 us
    pallas_call x1, Pallas kernels, on_device(): pl.pallas_call(hand_over, out_shape=(jax.ShapeDtypeStruct((nz, ny, nx), j...  1.31 us

profile of v2, /device:TPU:0, one launch (start us, length us, event | category | flops | bytes accessed | tf_op | source)
XLA Modules:
  0.0 29.0 jit_solution(13194756641802880618)
XLA Ops:
  0.6 27.1 %shard_map.41 = (f32[32,32,128]{2,1,0:T(8,128)S(1)}, f32[1,7]{1,0:T(1,128)S(1)}) custom-call(f32[7,32,32,128]{3,2,1,0:T(8,128)} %res.1, f32[7,32,32,128]{3,2,1,0:T(8,128)} %den.1), custom_call_target="tpu_custom_call" | custom-call | tf_op jit(solution)/shard_map/pallas_call | solution.py:358
  27.7 1.3 %shard_map.42 = (f32[32,32,128]{2,1,0:T(8,128)}, f32[1,7]{1,0:T(1,128)}) custom-call(f32[32,32,128]{2,1,0:T(8,128)S(1)} %get-tuple-element.6.mixed, f32[1,7]{1,0:T(1,128)S(1)} %get-tuple-element.7.weights), custom_call_target="tpu_custom_call" | custom-call | tf_op jit(solution)/shard_map/pallas_call | solution.py:382

commit v3 on v2

--- a/solution.py
+++ b/solution.py
@@ -11,7 +11,8 @@
 MESH = pl.DeviceIdType.MESH
 SWEEPS = 3
 SUB = 8
-UNROLL = 2
+UNROLL = 4
+DEEP = 16
 shift_value = 0.15
 mix_amount = 0.7
 AXES = ("gx", "gy", "gz")
@@ -34,7 +35,7 @@
 def kernel(
     counts, dims, chunks,
     res, den, out, wout,
-    held, dens, slots, comb, side, rhs_a, rhs_b, it_a, it_b, packs, landed, cpacks, clanded,
+    held, dens, slots, comb, rhs_a, it_a, strip, rhs_s, it_s, packs, landed, cfirst, clast,
     in_sem, den_sem, gsend, grecv, zsend, zrecv, ysend, yrecv, xsend, xrecv, csend, crecv,
 ):
     count, nz, ny, nx = dims
@@ -45,9 +46,6 @@
     ix, iy, iz = (lax.axis_index(a) for a in AXES)
     me = (ix * cy + iy) * cz + iz
 
-    def coords(flat):
-        return (flat // (cy * cz), lax.rem(flat // cz, cy), lax.rem(flat, cz))
-
     def near(dx, dy, dz):
         return (
             lax.rem(ix + dx + cx, cx),
@@ -68,10 +66,16 @@
 
     barrier = pltpu.get_barrier_semaphore()
 
-    @pl.loop(1, total_devices)
-    def _(k):
+    offsets = [
+        (dx, dy, dz) for dx in range(cx) for dy in range(cy) for dz in range(cz) if dx or dy or dz
+    ]
+    offsets.sort(key=lambda o: -sum(min(d, c - d) for d, c in zip(o, counts)))
+    gx = [lax.rem(ix + d, cx) for d in range(cx)]
+    gy = [lax.rem(iy + d, cy) for d in range(cy)]
+    gz = [lax.rem(iz + d, cz) for d in range(cz)]
+    for dx, dy, dz in offsets:
         pl.semaphore_signal(
-            barrier, inc=1, device_id=coords(lax.rem(me + k, total_devices)), device_id_type=MESH
+            barrier, inc=1, device_id=(gx[dx], gy[dy], gz[dz]), device_id_type=MESH
         )
 
     @pl.loop(h, ny + h)
@@ -101,19 +105,19 @@
 
     pl.semaphore_wait(barrier, total_devices - 1)
 
-    def gram_copy(k, slot, target):
+    def gram_copy(k, slot):
+        dx, dy, dz = offsets[k]
         return pltpu.make_async_remote_copy(
             src_ref=slots.at[me],
             dst_ref=slots.at[slot],
             send_sem=gsend.at[k],
-            recv_sem=grecv.at[slot],
-            device_id=coords(target),
+            recv_sem=grecv.at[k],
+            device_id=(gx[dx], gy[dy], gz[dz]),
             device_id_type=MESH,
         )
 
-    @pl.loop(1, total_devices)
-    def _(k):
-        gram_copy(k, me, lax.rem(me + k, total_devices)).start()
+    for k in range(len(offsets)):
+        gram_copy(k, me).start()
 
     zcopies = []
     for k, (start, dest, dz) in enumerate(((h, nz + h, -1), (nz, 0, 1))):
@@ -128,10 +132,9 @@
         cp.start()
         zcopies.append(cp)
 
-    @pl.loop(1, total_devices)
-    def _(k):
-        other = lax.rem(me + k, total_devices)
-        gram_copy(k, other, other).wait_recv()
+    for k, (dx, dy, dz) in enumerate(offsets):
+        source = (gx[-dx % cx] * cy + gy[-dy % cy]) * cz + gz[-dz % cz]
+        gram_copy(k, source).wait_recv()
 
     total = jnp.sum(slots[...], axis=0)
 
@@ -194,54 +197,76 @@
         cp.start()
         ycopies.append(cp)
 
-    group = lane // h
-
-    @pl.loop(0, zp // SUB)
-    def _(zt):
-        rows = pl.ds(pl.multiple_of(zt * SUB, SUB), SUB)
+    ztiles = zp // SUB
+    width = 6 * h
+    group = lane // width
+    inner = lane - width * group
+    at_left = inner < 3 * h
+
+    def own_strip(e):
+        total = jnp.zeros((SUB, nx), jnp.float32)
+        for zt in range(ztiles):
+            v = comb[e, zt * SUB:(zt + 1) * SUB, :]
+            near_left = pltpu.roll(v, (width * zt + h) % nx, 1)
+            near_right = pltpu.roll(v, (width * zt + 5 * h) % nx, 1)
+            total = jnp.where(group == zt, jnp.where(at_left, near_left, near_right), total)
+        strip[e] = total
+
+    def planes(start, stop, unroll):
+        steps = (stop - start) // unroll
+
+        def wrap(body):
+            @pl.loop(0, steps)
+            def _(it):
+                for r in range(unroll):
+                    body(start + it * unroll + r)
+
+            for e in range(start + steps * unroll, stop):
+                body(e)
+            return body
+
+        return wrap
+
+    planes(h, ny + h, 8)(own_strip)
+
+    each = width // h
+    place = inner // h
+    for m in range(packs.shape[1]):
         head = jnp.zeros((SUB, nx), jnp.float32)
         tail = jnp.zeros((SUB, nx), jnp.float32)
-        for y in range(ny):
-            v = comb[h + y, rows, :]
-            here = group == y
-            head = jnp.where(here, pltpu.roll(v, (h * y) % nx, 1), head)
-            tail = jnp.where(here, pltpu.roll(v, (h * y + h) % nx, 1), tail)
-        packs[0, rows, :] = head
-        packs[1, rows, :] = tail
-
+        for q in range(min(each, ny - m * each)):
+            v = strip[h + m * each + q]
+            head = jnp.where(place == q, pltpu.roll(v, (h * q - h) % nx, 1), head)
+            tail = jnp.where(place == q, pltpu.roll(v, (h * q - 4 * h) % nx, 1), tail)
+        packs[0, m] = head
+        packs[1, m] = tail
+
+    low = (ny - h) // each
     xcopies = []
-    for k, dx in enumerate((-1, 1)):
+
+    def send_x(source, target, send_sem, recv_sem, dx, dy):
         cp = pltpu.make_async_remote_copy(
-            src_ref=packs.at[k],
-            dst_ref=landed.at[k],
-            send_sem=xsend.at[k],
-            recv_sem=xrecv.at[k],
-            device_id=near(dx, 0, 0),
+            src_ref=source,
+            dst_ref=target,
+            send_sem=send_sem,
+            recv_sem=recv_sem,
+            device_id=near(dx, dy, 0),
             device_id_type=MESH,
         )
         cp.start()
         xcopies.append(cp)
-    span = h * h
-    corner_group = lane // span
+
     for k, dx in enumerate((-1, 1)):
-        for q, dy in enumerate((1, -1)):
-            first_lane = h * (ny - h) if dy > 0 else 0
-            corner = jnp.zeros((SUB, nx), jnp.float32)
-            for zt in range(zp // SUB):
-                v = packs[k, zt * SUB:(zt + 1) * SUB, :]
-                v = pltpu.roll(v, (span * zt - first_lane) % nx, 1)
-                corner = jnp.where(corner_group == zt, v, corner)
-            cpacks[k, q] = corner
-            cp = pltpu.make_async_remote_copy(
-                src_ref=cpacks.at[k, q],
-                dst_ref=clanded.at[k, q],
-                send_sem=csend.at[k, q],
-                recv_sem=crecv.at[k, q],
-                device_id=near(dx, dy, 0),
-                device_id_type=MESH,
-            )
-            cp.start()
-            xcopies.append(cp)
+        send_x(
+            packs.at[k, pl.ds(low, clast.shape[1])], clast.at[k],
+            csend.at[k, 0], crecv.at[k, 0], dx, 1,
+        )
+        send_x(
+            packs.at[k, pl.ds(0, cfirst.shape[1])], cfirst.at[k],
+            csend.at[k, 1], crecv.at[k, 1], dx, -1,
+        )
+    for k, dx in enumerate((-1, 1)):
+        send_x(packs.at[k], landed.at[k], xsend.at[k], xrecv.at[k], dx, 0)
 
     den_load.wait()
 
@@ -253,88 +278,113 @@
                 s = s + weights[i] * dens[i, z, t * SUB:(t + 1) * SUB, :]
             out[z, t * SUB:(t + 1) * SUB, :] = s
 
-    for cp in xcopies:
-        cp.wait()
-
-    left = lane < nx // 2
-
-    @pl.loop(0, zp // SUB)
-    def _(zt):
-        rows = pl.ds(pl.multiple_of(zt * SUB, SUB), SUB)
-        for y in range(ny):
-            head = pltpu.roll(landed[0, rows, :], (-h * y) % nx, 1)
-            tail = pltpu.roll(landed[1, rows, :], (nx - h - h * y) % nx, 1)
-            side[h + y, rows, :] = jnp.where(left, head, tail)
-
-    for q, base in ((0, 0), (1, ny + h)):
-        for zt in range(zp // SUB):
-            for r in range(h):
-                at = span * zt + h * r
-                head = pltpu.roll(clanded[0, q], (-at) % nx, 1)
-                tail = pltpu.roll(clanded[1, q], (nx - h - at) % nx, 1)
-                side[base + r, zt * SUB:(zt + 1) * SUB, :] = jnp.where(left, head, tail)
-
-    for cp in ycopies:
-        cp.wait()
-
-    wide = lax.broadcasted_iota(jnp.int32, (zp, nx), 1)
-    first, last = wide == 0, wide == nx - 1
-
-    def around(fa, fb, e, both):
-        a, s = fa[e], fb[e]
-        ra, rs = pltpu.roll(a, 1, 1), pltpu.roll(s, 1, 1)
-        la, ls = pltpu.roll(a, nx - 1, 1), pltpu.roll(s, nx - 1, 1)
-        na = jnp.where(first, rs, ra) + jnp.where(last, ls, la)
-        na = na + (pltpu.roll(a, 1, 0) + pltpu.roll(a, zp - 1, 0))
-        na = na + (fa[e - 1] + fa[e + 1])
-        if not both:
-            return a, na
-        ns = jnp.where(first, ra, rs) + jnp.where(last, la, ls)
-        ns = ns + (pltpu.roll(s, 1, 0) + pltpu.roll(s, zp - 1, 0))
-        ns = ns + (fb[e - 1] + fb[e + 1])
-        return a, na, s, ns
+    def around(f, e):
+        v = f[e]
+        total = pltpu.roll(v, 1, 1) + pltpu.roll(v, nx - 1, 1)
+        total = total + (pltpu.roll(v, 1, 0) + pltpu.roll(v, zp - 1, 0))
+        return v, total + (f[e - 1] + f[e + 1])
 
     diag_value = 6.0 + shift_value
     w1, w2, w3 = sweep_weights()
     alpha = ((1.0 - w2) * w1 + w2) / diag_value
     beta = w1 * w2 / (diag_value * diag_value)
 
-    def planes(start, stop, unroll):
-        unroll = unroll if (stop - start) % unroll == 0 else 1
-
-        def wrap(body):
-            @pl.loop(0, (stop - start) // unroll)
-            def _(it):
-                for r in range(unroll):
-                    body(start + it * unroll + r)
-
-        return wrap
-
-    @planes(1, ny + 2 * h - 1, UNROLL)
-    def _(e):
-        a, na, s, ns = around(comb, side, e, True)
-        rhs_a[e] = 6.0 * a - na
-        rhs_b[e] = 6.0 * s - ns
-
-    @planes(2, ny + 2 * h - 2, UNROLL)
-    def _(e):
-        a, na, s, ns = around(rhs_a, rhs_b, e, True)
-        it_a[e] = alpha * a + beta * na
-        it_b[e] = alpha * s + beta * ns
+    def first_pass(e):
+        v, total = around(comb, e)
+        rhs_a[e] = 6.0 * v - total
+
+    planes(h + 1, ny + h - 1, UNROLL)(first_pass)
+
+    def second_pass(e):
+        v, total = around(rhs_a, e)
+        it_a[e] = alpha * v + beta * total
+
+    planes(h + 2, ny + h - 2, UNROLL)(second_pass)
 
     out_flat = out.reshape(nz * ny, nx)
-
-    @planes(3, ny + 2 * h - 3, UNROLL)
-    def _(e):
-        a, na = around(it_a, it_b, e, False)
-        u = (mix_amount * (1.0 - w3)) * a + (mix_amount * w3 / diag_value) * (rhs_a[e] + na)
+    edge = (lane < h) | (lane >= nx - h)
+
+    def last_step(v, total, r):
+        return (mix_amount * (1.0 - w3)) * v + (mix_amount * w3 / diag_value) * (r + total)
+
+    def third_pass(e):
+        v, total = around(it_a, e)
+        u = last_step(v, total, rhs_a[e])
         for zt in range(nz // SUB):
             rows = pl.ds(zt * SUB * ny + (e - h), SUB, stride=ny)
-            out_flat[rows, :] = out_flat[rows, :] + u[zt * SUB:(zt + 1) * SUB, :]
-
-    @pl.loop(1, total_devices)
-    def _(k):
-        gram_copy(k, me, lax.rem(me + k, total_devices)).wait_send()
+            part = u[zt * SUB:(zt + 1) * SUB, :]
+            out_flat[rows, :] = out_flat[rows, :] + jnp.where(edge, 0.0, part)
+
+    planes(h + 3, ny + h - 3, UNROLL)(third_pass)
+
+    for cp in ycopies:
+        cp.wait()
+
+    for e in (*range(h), *range(ny + h, ny + 2 * h)):
+        own_strip(e)
+    for e in (*range(1, h + 1), *range(ny + h - 1, ny + 2 * h - 1)):
+        first_pass(e)
+    for e in (*range(2, h + 2), *range(ny + h - 2, ny + 2 * h - 2)):
+        second_pass(e)
+    for e in (*range(h, h + 3), *range(ny + h - 3, ny + h)):
+        third_pass(e)
+
+    for cp in xcopies:
+        cp.wait()
+
+    for e in range(ny + 2 * h):
+        if e < h:
+            ref, y, m0 = clast, ny - h + e, low
+        elif e < ny + h:
+            ref, y, m0 = landed, e - h, 0
+        else:
+            ref, y, m0 = cfirst, e - h - ny, 0
+        m, q = y // each - m0, y % each
+        head = pltpu.roll(ref[0, m], (5 * h - h * q) % nx, 1)
+        tail = pltpu.roll(ref[1, m], (-h * q) % nx, 1)
+        strip[e] = jnp.where(inner < h, tail, jnp.where(inner >= 5 * h, head, strip[e]))
+
+    sub = lax.broadcasted_iota(jnp.int32, (SUB, nx), 0)
+    wrap_by = (ztiles - 1) * width
+
+    def around_strip(f, e):
+        v = f[e]
+        total = pltpu.roll(v, 1, 1) + pltpu.roll(v, nx - 1, 1)
+        below = pltpu.roll(v, 1, 0)
+        carried = jnp.where(
+            group == 0, pltpu.roll(below, nx - wrap_by, 1), pltpu.roll(below, width, 1)
+        )
+        total = total + jnp.where(sub == 0, carried, below)
+        above = pltpu.roll(v, SUB - 1, 0)
+        carried = jnp.where(
+            group == ztiles - 1, pltpu.roll(above, wrap_by, 1), pltpu.roll(above, nx - width, 1)
+        )
+        total = total + jnp.where(sub == SUB - 1, carried, above)
+        return v, total + (f[e - 1] + f[e + 1])
+
+    @planes(1, ny + 2 * h - 1, DEEP)
+    def _(e):
+        v, total = around_strip(strip, e)
+        rhs_s[e] = 6.0 * v - total
+
+    @planes(2, ny + 2 * h - 2, DEEP)
+    def _(e):
+        v, total = around_strip(rhs_s, e)
+        it_s[e] = alpha * v + beta * total
+
+    @planes(h, ny + h, DEEP)
+    def _(e):
+        v, total = around_strip(it_s, e)
+        u = last_step(v, total, rhs_s[e])
+        for zt in range(nz // SUB):
+            rows = pl.ds(zt * SUB * ny + (e - h), SUB, stride=ny)
+            from_left = pltpu.roll(u, (-(width * zt + h)) % nx, 1)
+            from_right = pltpu.roll(u, (-5 * h - width * zt) % nx, 1)
+            part = jnp.where(lane < nx // 2, from_left, from_right)
+            out_flat[rows, :] = out_flat[rows, :] + jnp.where(edge, part, 0.0)
+
+    for k in range(len(offsets)):
+        gram_copy(k, me).wait_send()
 
 
 def hand_over(mixed, weights, out, wout, sem):
@@ -352,7 +402,14 @@
     n = counts[0] * counts[1] * counts[2]
     chunks = 4
     field = pltpu.VMEM((ny + 2 * h, zp, nx), jnp.float32)
+    strips = pltpu.VMEM((ny + 2 * h, SUB, nx), jnp.float32)
+    each = 6
+    messages = pl.cdiv(ny, each)
     dma = pltpu.SemaphoreType.DMA
+
+    def faces(blocks):
+        return pltpu.VMEM((2, blocks, SUB, nx), jnp.float32)
+
     any_spec = pl.BlockSpec(memory_space=pl.ANY)
     vmem = pl.BlockSpec(memory_space=pltpu.VMEM)
     new_density, weights = pl.pallas_call(
@@ -367,11 +424,11 @@
             pltpu.VMEM((count, nz + 2 * h, ny, nx), jnp.float32),
             pltpu.VMEM(dims, jnp.float32),
             pltpu.VMEM((n, 1, nx), jnp.float32),
-            field, field, field, field, field, field,
-            pltpu.VMEM((2, zp, nx), jnp.float32),
-            pltpu.VMEM((2, zp, nx), jnp.float32),
-            pltpu.VMEM((2, 2, SUB, nx), jnp.float32),
-            pltpu.VMEM((2, 2, SUB, nx), jnp.float32),
+            field, field, field, strips, strips, strips,
+            faces(messages),
+            faces(messages),
+            faces(pl.cdiv(h, each)),
+            faces(messages - (ny - h) // each),
             dma((chunks,)), dma(()), dma((n,)), dma((n,)),
             dma((2,)), dma((2,)), dma((2,)), dma((2,)), dma((2,)), dma((2,)), dma((2, 2)), dma((2, 2)),
         ],

time: 29.2 us -> 24.7 us (0.85)
  Pallas kernels: 28.4 us -> 23.9 us
    pallas_call x1, Pallas kernels: 27.1 us -> 22.6 us  [on_device(): pl.pallas_call(functools.partial(kernel, counts, dims, chunks), out_shape...]
where the time goes in v3:
time: 24.7 us; the launch traced here: 24.5 us
  Pallas kernels  23.9 us (97%)
  between operations  0.64 us (3%)
    pallas_call x1, Pallas kernels, on_device(): pl.pallas_call(functools.partial(kernel, counts, dims, chunks), out_shape...  22.6 us
    pallas_call x1, Pallas kernels, on_device(): pl.pallas_call(hand_over, out_shape=(jax.ShapeDtypeStruct((nz, ny, nx), j...  1.31 us

profile of v3, /device:TPU:0, one launch (start us, length us, event | category | flops | bytes accessed | tf_op | source)
XLA Modules:
  0.0 24.5 jit_solution(16761998475453791507)
XLA Ops:
  0.6 22.6 %shard_map.41 = (f32[32,32,128]{2,1,0:T(8,128)S(1)}, f32[1,7]{1,0:T(1,128)S(1)}) custom-call(f32[7,32,32,128]{3,2,1,0:T(8,128)} %res.1, f32[7,32,32,128]{3,2,1,0:T(8,128)} %den.1), custom_call_target="tpu_custom_call" | custom-call | tf_op jit(solution)/shard_map/pallas_call | solution.py:415
  23.2 1.3 %shard_map.42 = (f32[32,32,128]{2,1,0:T(8,128)}, f32[1,7]{1,0:T(1,128)}) custom-call(f32[32,32,128]{2,1,0:T(8,128)S(1)} %get-tuple-element.6.mixed, f32[1,7]{1,0:T(1,128)S(1)} %get-tuple-element.7.weights), custom_call_target="tpu_custom_call" | custom-call | tf_op jit(solution)/shard_map/pallas_call | solution.py:439

commit v4 on v3

--- a/solution.py
+++ b/solution.py
@@ -35,7 +35,7 @@
 def kernel(
     counts, dims, chunks,
     res, den, out, wout,
-    held, dens, slots, comb, rhs_a, it_a, strip, rhs_s, it_s, packs, landed, cfirst, clast,
+    held, dens, slots, comb, rhs_a, it_a, final, faces, strip, rhs_s, it_s, packs, landed, cfirst, clast,
     in_sem, den_sem, gsend, grecv, zsend, zrecv, ysend, yrecv, xsend, xrecv, csend, crecv,
 ):
     count, nz, ny, nx = dims
@@ -184,19 +184,6 @@
         combine(j, zp - h + j)
         combine(nz + h + j, nz + j)
 
-    ycopies = []
-    for k, (start, dest, dy) in enumerate(((h, ny + h, -1), (ny, 0, 1))):
-        cp = pltpu.make_async_remote_copy(
-            src_ref=comb.at[pl.ds(start, h)],
-            dst_ref=comb.at[pl.ds(dest, h)],
-            send_sem=ysend.at[k],
-            recv_sem=yrecv.at[k],
-            device_id=near(0, dy, 0),
-            device_id_type=MESH,
-        )
-        cp.start()
-        ycopies.append(cp)
-
     ztiles = zp // SUB
     width = 6 * h
     group = lane // width
@@ -268,6 +255,19 @@
     for k, dx in enumerate((-1, 1)):
         send_x(packs.at[k], landed.at[k], xsend.at[k], xrecv.at[k], dx, 0)
 
+    ycopies = []
+    for k, (start, dest, dy) in enumerate(((h, ny + h, -1), (ny, 0, 1))):
+        cp = pltpu.make_async_remote_copy(
+            src_ref=comb.at[pl.ds(start, h)],
+            dst_ref=comb.at[pl.ds(dest, h)],
+            send_sem=ysend.at[k],
+            recv_sem=yrecv.at[k],
+            device_id=near(0, dy, 0),
+            device_id_type=MESH,
+        )
+        cp.start()
+        ycopies.append(cp)
+
     den_load.wait()
 
     @pl.loop(0, nz)
@@ -301,7 +301,6 @@
 
     planes(h + 2, ny + h - 2, UNROLL)(second_pass)
 
-    out_flat = out.reshape(nz * ny, nx)
     edge = (lane < h) | (lane >= nx - h)
 
     def last_step(v, total, r):
@@ -311,9 +310,8 @@
         v, total = around(it_a, e)
         u = last_step(v, total, rhs_a[e])
         for zt in range(nz // SUB):
-            rows = pl.ds(zt * SUB * ny + (e - h), SUB, stride=ny)
-            part = u[zt * SUB:(zt + 1) * SUB, :]
-            out_flat[rows, :] = out_flat[rows, :] + jnp.where(edge, 0.0, part)
+            rows = slice(zt * SUB, (zt + 1) * SUB)
+            final[e, rows, :] = u[rows, :]
 
     planes(h + 3, ny + h - 3, UNROLL)(third_pass)
 
@@ -372,26 +370,43 @@
         v, total = around_strip(rhs_s, e)
         it_s[e] = alpha * v + beta * total
 
-    @planes(h, ny + h, DEEP)
-    def _(e):
+    def last_strips(e):
         v, total = around_strip(it_s, e)
         u = last_step(v, total, rhs_s[e])
+        u = jnp.where(inner < h, pltpu.roll(u, nx - 4 * h, 1), u)
         for zt in range(nz // SUB):
-            rows = pl.ds(zt * SUB * ny + (e - h), SUB, stride=ny)
-            from_left = pltpu.roll(u, (-(width * zt + h)) % nx, 1)
-            from_right = pltpu.roll(u, (-5 * h - width * zt) % nx, 1)
-            part = jnp.where(lane < nx // 2, from_left, from_right)
-            out_flat[rows, :] = out_flat[rows, :] + jnp.where(edge, part, 0.0)
+            faces[e, zt * SUB:(zt + 1) * SUB, :] = pltpu.roll(u, (-(width * zt + h)) % nx, 1)
+
+    planes(h, ny + h, DEEP)(last_strips)
+
+    flat_final = final.reshape((ny + 2 * h) * zp, nx)
+    flat_faces = faces.reshape((ny + 2 * h) * zp, nx)
+
+    @pl.loop(0, nz // 4)
+    def _(block):
+        for r in range(4):
+            z = block * 4 + r
+            for t in range(tiles):
+                rows = pl.ds((h + t * SUB) * zp + z, SUB, stride=zp)
+                u = jnp.where(edge, flat_faces[rows, :], flat_final[rows, :])
+                out[z, t * SUB:(t + 1) * SUB, :] = out[z, t * SUB:(t + 1) * SUB, :] + u
 
     for k in range(len(offsets)):
         gram_copy(k, me).wait_send()
 
 
 def hand_over(mixed, weights, out, wout, sem):
-    cp = pltpu.make_async_copy(mixed, out, sem)
-    cp.start()
+    pieces = sem.shape[0]
+    per = mixed.shape[0] // pieces
+    copies = []
+    for c in range(pieces):
+        part = pl.ds(c * per, per)
+        cp = pltpu.make_async_copy(mixed.at[part], out.at[part], sem.at[c])
+        cp.start()
+        copies.append(cp)
     wout[...] = weights[...]
-    cp.wait()
+    for cp in copies:
+        cp.wait()
 
 
 def on_device(counts, densities, residuals):
@@ -424,7 +439,7 @@
             pltpu.VMEM((count, nz + 2 * h, ny, nx), jnp.float32),
             pltpu.VMEM(dims, jnp.float32),
             pltpu.VMEM((n, 1, nx), jnp.float32),
-            field, field, field, strips, strips, strips,
+            field, field, field, field, field, strips, strips, strips,
             faces(messages),
             faces(messages),
             faces(pl.cdiv(h, each)),
@@ -444,7 +459,7 @@
         ),
         in_specs=[vmem, vmem],
         out_specs=(any_spec, vmem),
-        scratch_shapes=[dma(())],
+        scratch_shapes=[dma((4,))],
         compiler_params=pltpu.CompilerParams(vmem_limit_bytes=4 * 1024 * 1024),
     )(new_density, weights)
     return new_density, weights.reshape(count)

time: 24.7 us -> 23.3 us (0.943)
  Pallas kernels: 23.9 us -> 22.5 us
    pallas_call x1, Pallas kernels: 22.6 us -> 21.1 us  [on_device(): pl.pallas_call(functools.partial(kernel, counts, dims, chunks), out_shape...]
where the time goes in v4:
time: 23.3 us; the launch traced here: 23.1 us
  Pallas kernels  22.5 us (97%)
  between operations  0.64 us (3%)
    pallas_call x1, Pallas kernels, on_device(): pl.pallas_call(functools.partial(kernel, counts, dims, chunks), out_shape...  21.1 us
    pallas_call x1, Pallas kernels, on_device(): pl.pallas_call(hand_over, out_shape=(jax.ShapeDtypeStruct((nz, ny, nx), j...  1.33 us

profile of v4, /device:TPU:0, one launch (start us, length us, event | category | flops | bytes accessed | tf_op | source)
XLA Modules:
  0.0 23.1 jit_solution(10036473987067922)
XLA Ops:
  0.6 21.1 %shard_map.41 = (f32[32,32,128]{2,1,0:T(8,128)S(1)}, f32[1,7]{1,0:T(1,128)S(1)}) custom-call(f32[7,32,32,128]{3,2,1,0:T(8,128)} %res.1, f32[7,32,32,128]{3,2,1,0:T(8,128)} %den.1), custom_call_target="tpu_custom_call" | custom-call | tf_op jit(solution)/shard_map/pallas_call | solution.py:430
  21.8 1.3 %shard_map.42 = (f32[32,32,128]{2,1,0:T(8,128)}, f32[1,7]{1,0:T(1,128)}) custom-call(f32[32,32,128]{2,1,0:T(8,128)S(1)} %get-tuple-element.6.mixed, f32[1,7]{1,0:T(1,128)S(1)} %get-tuple-element.7.weights), custom_call_target="tpu_custom_call" | custom-call | tf_op jit(solution)/shard_map/pallas_call | solution.py:454
